TPU v7x, 32 devices: a whole 2x2x4 slice. The times are simulated.
32 devices in a mesh: gx: 4 (over y, x), gy: 2 (over core), gz: 4 (over z).
Axes of the slice: x: 2, y: 2, z: 4, core: 2. Of those that a mesh axis runs over, the one named last changes fastest.
Arguments:
- right_side: float32 [8, 32, 64, 512], P(None, 'gx', 'gy', 'gz'), may hold values from -12 to 12
- shift: float32 [32, 64, 512], P('gx', 'gy', 'gz'), may hold values from 0.02 to 2
Outputs:
- solution_block: float32 [8, 32, 64, 512], P(None, 'gx', 'gy', 'gz')
- residual_norms: float32 [8], replicated
All inputs are finite; a program needn't handle non-finite values.
Results may differ from a plain program's by a relative error of at most 0.0003.
Values sent between devices are 32-bit elements; how exact they have to be, the bound alone decides.
No kernel may reach another device: no remote copies, remote signals or barrier semaphores. Data moves between devices by JAX's collectives and lax.ppermute only.
A program may use at most 128 MiB of HBM per device.

v0:
```python
import jax
import jax.numpy as jnp
from jax import lax
from jax.sharding import PartitionSpec as P

ITERS = 2


def padded_2(block, sides, width):
    for axis, dim in sides:
        count = lax.axis_size(axis)
        forward = [(i, i + 1) for i in range(count - 1)]
        backward = [(target, source) for source, target in forward]
        low = lax.ppermute(
            lax.slice_in_dim(block, block.shape[dim] - width, None, axis=dim), axis, forward
        )
        high = lax.ppermute(lax.slice_in_dim(block, 0, width, axis=dim), axis, backward)
        block = jnp.concatenate([low, block, high], axis=dim)
    return block


def operate(fields, shift):
    padded = padded_2(fields, (("gx", 1), ("gy", 2), ("gz", 3)), 1)
    beside = padded[:, 2:, 1:-1, 1:-1] + padded[:, :-2, 1:-1, 1:-1]
    beside = beside + padded[:, 1:-1, 2:, 1:-1] + padded[:, 1:-1, :-2, 1:-1]
    beside = beside + padded[:, 1:-1, 1:-1, 2:] + padded[:, 1:-1, 1:-1, :-2]
    return (6.0 + shift)[None] * fields - beside


def lower_inverse(lower):
    count = lower.shape[0]
    return jax.scipy.linalg.solve_triangular(lower, jnp.eye(count, dtype=lower.dtype), lower=True)


def small_dot(left, right):
    return jnp.dot(left, right, precision=lax.Precision.HIGHEST)


def body(right_side, shift):
    width = right_side.shape[0]
    shape = right_side.shape
    rows = right_side.reshape(width, -1)
    gram = lax.psum(small_dot(rows, rows.T), ("gx", "gy", "gz"))
    lower = jnp.linalg.cholesky(gram)
    start_coeff = lower.T
    basis = [small_dot(lower_inverse(lower), rows)]
    hessen = jnp.zeros(((ITERS + 1) * width, ITERS * width), jnp.float32)
    for step in range(ITERS):
        image = operate(basis[step].reshape(shape), shift).reshape(width, -1)
        stacked = jnp.concatenate(basis, axis=0)
        products = lax.psum(
            small_dot(jnp.concatenate([stacked, image], axis=0), image.T), ("gx", "gy", "gz")
        )
        coeffs = products[:-width]
        gram = products[-width:] - small_dot(coeffs.T, coeffs)
        projected = image - small_dot(coeffs.T, stacked)
        lower = jnp.linalg.cholesky(gram)
        hessen = hessen.at[: (step + 1) * width, step * width : (step + 1) * width].set(coeffs)
        hessen = hessen.at[
            (step + 1) * width : (step + 2) * width, step * width : (step + 1) * width
        ].set(lower.T)
        if step + 1 < ITERS:
            basis.append(small_dot(lower_inverse(lower), projected))
    target = jnp.zeros(((ITERS + 1) * width, width), jnp.float32).at[:width].set(start_coeff)
    normal = small_dot(hessen.T, hessen)
    factor = jnp.linalg.cholesky(normal)
    coeff_y = jax.scipy.linalg.cho_solve((factor, True), small_dot(hessen.T, target))
    solution = small_dot(coeff_y.T, jnp.concatenate(basis, axis=0)).reshape(shape)
    leftover = target - small_dot(hessen, coeff_y)
    norms = jnp.sqrt(jnp.sum(leftover * leftover, axis=0))
    return (solution, norms)


def solution(mesh):
    in_specs = (P(None, "gx", "gy", "gz"), P("gx", "gy", "gz"))
    out_specs = (P(None, "gx", "gy", "gz"), P())
    return jax.shard_map(body, mesh=mesh, in_specs=in_specs, out_specs=out_specs, check_vma=False)
```

profile of v0, /device:TPU:0, one launch (start us, length us, event | category | flops | bytes accessed | tf_op | source)
XLA Modules:
  0.0 228.1 jit_solution(12695287434098205644)
XLA Ops:
  0.6 4.9 %convolution_bitcast_fusion = f32[8,8]{0,1:T(8,128)S(1)} fusion(f32[8,8,32,128]{3,2,1,0:T(8,128)} %param.15), kind=kOutput, calls=%fused_computation.19 | convolution fusion | flops 25165824 | bytes 1048832 | tf_op jit(solution)/shard_map/dot_general | solution.py:36
  5.5 42.0 %psum.21 = f32[8,8]{0,1:T(8,128)S(1)} all-reduce(f32[8,8]{0,1:T(8,128)S(1)} %convolution_bitcast_fusion), channel_id=1, replica_groups=mesh['gx'=4,'gy'=2,'gz'=4] {'gx','gy','gz'}, use_global_device_ids=true, to_apply=%region_0.0 | all-reduce | flops 64 | bytes 512 | tf_op jit(solution)/shard_map/psum | solution.py:43
  50.4 1.5 fusion.12
  51.9 1.3 collective-permute-start
  53.2 4.8 %collective-permute-start.1 = (f32[8,1,32,128]{3,0,2,1:T(8,128)S(1)}, f32[8,1,32,128]{3,0,2,1:T(8,128)S(1)}, u32[]{:S(2)}, u32[]{:S(2)}) collective-permute-start(f32[8,1,32,128]{3,0,2,1:T(8,128)S(1)} %get-tuple-element.84), channel_id=1, source_target_pairs={{0,8},{8,16},{16,24},{1,9},{9,17},{17,25},{2,10},{10,18},{18,26},{... | collective-permute-start | bytes 393224 | tf_op jit(solution)/shard_map/ppermute | solution.py:14
  59.1 1.5 collective-permute-done.1
  60.6 1.3 collective-permute-start.2
  61.9 3.0 %collective-permute-start.3 = (f32[8,10,1,128]{3,0,2,1:T(8,128)S(1)}, f32[8,10,1,128]{3,0,2,1:T(8,128)S(1)}, u32[]{:S(2)}, u32[]{:S(2)}) collective-permute-start(f32[8,10,1,128]{3,0,2,1:T(8,128)S(1)} %get-tuple-element.80), channel_id=1, source_target_pairs={{0,4},{1,5},{2,6},{3,7},{8,12},{9,13},{10,14},{11,15},{16,20},{17,... | collective-permute-start | bytes 122888 | tf_op jit(solution)/shard_map/ppermute | solution.py:14
  66.4 1.5 fusion.56
  67.9 2.0 copy.130
  70.0 1.3 collective-permute-start.4
  71.9 4.5 %collective-permute-start.5 = (f32[8,10,34,1]{2,0,3,1:T(8,128)S(1)}, f32[8,10,34,1]{2,0,3,1:T(8,128)S(1)}, u32[]{:S(2)}, u32[]{:S(2)}) collective-permute-start(f32[8,10,34,1]{2,0,3,1:T(8,128)S(1)} %copy.132), channel_id=1, source_target_pairs={{0,1},{1,2},{2,3},{4,5},{5,6},{6,7},{8,9},{9,10},{10,11},{12,13},{... | collective-permute-start | bytes 32648 | tf_op jit(solution)/shard_map/ppermute | solution.py:14
  78.1 1.8 copy.133
  79.9 3.0 %fusion.22 = f32[8,8,32,128]{3,0,2,1:T(8,128)S(1)} fusion(f32[8,10,34,1]{3,0,2,1:T(8,128)} %copy.133, f32[8,10,1,128]{3,0,2,1:T(8,128)S(1)} %collective-permute-done.2, f32[8,10,1,128]{3,0,2,1:T(8,128)} %copy-done.6, f32[8,1,32,128]{3,0,2,1:T(8,128)} %copy-done.3, f32[8,8,32,128]{3,0,2,1:T(8,128)S(1)} %bitcast.73, f32[8,1,32,128]{3,0,2,1:T(8,128)} %copy-done.4, ...), kind=kLoop, calls=%fused_computation.50 | loop fusion | flops 6553600 | bytes 2594048 | tf_op jit(solution)/shard_map/sub | solution.py:27
  82.9 2.6 %fusion.6 = f32[16,8]{0,1:T(8,128)S(1)} fusion(f32[8,32768]{1,0:T(8,128)S(1)} %bitcast.78, f32[8,32768]{1,0:T(8,128)S(1)} %fusion.12), kind=kOutput, calls=%fused_computation.9 | convolution fusion | flops 50855936 | bytes 2097664 | tf_op jit(solution)/shard_map/dot_general | solution.py:36
  85.5 43.2 %psum.22 = f32[16,8]{0,1:T(8,128)S(1)} all-reduce(f32[16,8]{0,1:T(8,128)S(1)} %fusion.6), channel_id=1, replica_groups=mesh['gx'=4,'gy'=2,'gz'=4] {'gx','gy','gz'}, use_global_device_ids=true, to_apply=%region_3.0 | all-reduce | flops 128 | bytes 1024 | tf_op jit(solution)/shard_map/psum | solution.py:51
  133.7 1.3 collective-permute-start.6
  135.0 4.8 %collective-permute-start.7 = (f32[8,1,32,128]{3,0,2,1:T(8,128)S(1)}, f32[8,1,32,128]{3,0,2,1:T(8,128)S(1)}, u32[]{:S(2)}, u32[]{:S(2)}) collective-permute-start(f32[8,1,32,128]{3,0,2,1:T(8,128)S(1)} %get-tuple-element.82), channel_id=1, source_target_pairs={{0,8},{8,16},{16,24},{1,9},{9,17},{17,25},{2,10},{10,18},{18,26},{... | collective-permute-start | bytes 393224 | tf_op jit(solution)/shard_map/ppermute | solution.py:14
  141.1 1.3 collective-permute-done.7
  142.4 1.3 collective-permute-start.8
  143.7 3.0 %collective-permute-start.9 = (f32[8,10,1,128]{3,0,2,1:T(8,128)S(1)}, f32[8,10,1,128]{3,0,2,1:T(8,128)S(1)}, u32[]{:S(2)}, u32[]{:S(2)}) collective-permute-start(f32[8,10,1,128]{3,0,2,1:T(8,128)S(1)} %get-tuple-element.78), channel_id=1, source_target_pairs={{0,4},{1,5},{2,6},{3,7},{8,12},{9,13},{10,14},{11,15},{16,20},{17,... | collective-permute-start | bytes 122888 | tf_op jit(solution)/shard_map/ppermute | solution.py:14
  148.3 1.5 fusion.55
  149.8 2.6 %copy.137 = f32[8,10,34,1]{2,0,3,1:T(8,128)} copy(f32[8,10,34,1]{3,0,2,1:T(8,128)} %get-tuple-element.74) | data formatting | bytes 21760 | tf_op jit(solution)/shard_map/slice | solution.py:17
  155.0 5.2 %collective-permute-start.11 = (f32[8,10,34,1]{2,0,3,1:T(8,128)}, f32[8,10,34,1]{2,0,3,1:T(8,128)}, u32[]{:S(2)}, u32[]{:S(2)}) collective-permute-start(f32[8,10,34,1]{2,0,3,1:T(8,128)} %copy.139), channel_id=1, source_target_pairs={{0,1},{1,2},{2,3},{4,5},{5,6},{6,7},{8,9},{9,10},{10,11},{12,13},{... | collective-permute-start | bytes 32648 | tf_op jit(solution)/shard_map/ppermute | solution.py:14
  161.8 1.5 copy.138
  163.3 2.6 %copy.140 = f32[8,10,34,1]{3,0,2,1:T(8,128)} copy(f32[8,10,34,1]{2,0,3,1:T(8,128)} %collective-permute-done.11) | data formatting | bytes 21760 | tf_op jit(solution)/shard_map/ppermute | solution.py:14
  165.8 3.0 %fusion.16 = f32[8,8,32,128]{3,0,2,1:T(8,128)S(1)} fusion(f32[8,10,34,1]{3,0,2,1:T(8,128)} %copy.140, f32[8,10,1,128]{3,0,2,1:T(8,128)S(1)} %collective-permute-done.8, f32[8,10,1,128]{3,0,2,1:T(8,128)} %copy-done.5, f32[8,1,32,128]{3,0,2,1:T(8,128)} %copy-done.1, f32[8,8,32,128]{3,0,2,1:T(8,128)S(1)} %bitcast.77, f32[8,1,32,128]{3,0,2,1:T(8,128)} %copy-done.2, ...), kind=kLoop, calls=%fused_computation.26 | loop fusion | flops 6553600 | bytes 2594048 | tf_op jit(solution)/shard_map/sub | solution.py:27
  168.9 3.0 %fusion = f32[24,8]{0,1:T(8,128)S(1)} fusion(f32[8,32768]{1,0:T(8,128)S(1)} %bitcast.82, f32[8,32768]{1,0:T(8,128)S(1)} %fusion.60, f32[8,32768]{1,0:T(8,128)S(1)} %fusion.12), kind=kOutput, calls=%fused_computation.1 | convolution fusion | flops 77070336 | bytes 3146496 | tf_op jit(solution)/shard_map/dot_general | solution.py:36
  171.9 42.0 %psum.23 = f32[24,8]{0,1:T(8,128)S(1)} all-reduce(f32[24,8]{0,1:T(8,128)S(1)} %fusion), channel_id=1, replica_groups=mesh['gx'=4,'gy'=2,'gz'=4] {'gx','gy','gz'}, use_global_device_ids=true, to_apply=%region_5.0 | all-reduce | flops 192 | bytes 1536 | tf_op jit(solution)/shard_map/psum | solution.py:51
  216.1 2.0 dynamic-slice_select_fusion
  218.1 1.7 scatter.20
  220.6 1.5 cholesky.41
  (83 shorter events, 28.8 us)
Async XLA Ops:
  0.6 49.8 %copy-start = (f32[8,8,32,128]{3,2,1,0:T(8,128)S(1)}, f32[8,8,32,128]{3,2,1,0:T(8,128)}, u32[]{:S(2)}) copy-start(f32[8,8,32,128]{3,2,1,0:T(8,128)} %param.15) | copy-start | bytes 3145732
  51.9 7.1 %collective-permute-start = (f32[8,1,32,128]{3,0,2,1:T(8,128)S(1)}, f32[8,1,32,128]{3,0,2,1:T(8,128)S(1)}, u32[]{:S(2)}, u32[]{:S(2)}) collective-permute-start(f32[8,1,32,128]{3,0,2,1:T(8,128)S(1)} %get-tuple-element.85), channel_id=1, source_target_pairs={{8,0},{16,8},{24,16},{9,1},{17,9},{25,17},{10,2},{18,10},{26,18},{... | collective-permute-start | bytes 393224 | tf_op jit(solution)/shard_map/ppermute | solution.py:17
  53.2 7.3 %collective-permute-start.1 = (f32[8,1,32,128]{3,0,2,1:T(8,128)S(1)}, f32[8,1,32,128]{3,0,2,1:T(8,128)S(1)}, u32[]{:S(2)}, u32[]{:S(2)}) collective-permute-start(f32[8,1,32,128]{3,0,2,1:T(8,128)S(1)} %get-tuple-element.84), channel_id=1, source_target_pairs={{0,8},{8,16},{16,24},{1,9},{9,17},{17,25},{2,10},{10,18},{18,26},{... | collective-permute-start | bytes 393224 | tf_op jit(solution)/shard_map/ppermute | solution.py:14
  59.1 6.8 %copy-start.3 = (f32[8,1,32,128]{3,0,2,1:T(8,128)}, f32[8,1,32,128]{3,0,2,1:T(8,128)S(1)}, u32[]{:S(2)}) copy-start(f32[8,1,32,128]{3,0,2,1:T(8,128)S(1)} %collective-permute-done) | copy-start | bytes 393220
  60.6 5.3 %copy-start.4 = (f32[8,1,32,128]{3,0,2,1:T(8,128)}, f32[8,1,32,128]{3,0,2,1:T(8,128)S(1)}, u32[]{:S(2)}) copy-start(f32[8,1,32,128]{3,0,2,1:T(8,128)S(1)} %collective-permute-done.1) | copy-start | bytes 393220
  60.6 4.3 %collective-permute-start.2 = (f32[8,10,1,128]{3,0,2,1:T(8,128)S(1)}, f32[8,10,1,128]{3,0,2,1:T(8,128)S(1)}, u32[]{:S(2)}, u32[]{:S(2)}) collective-permute-start(f32[8,10,1,128]{3,0,2,1:T(8,128)S(1)} %get-tuple-element.81), channel_id=1, source_target_pairs={{4,0},{5,1},{6,2},{7,3},{12,8},{13,9},{14,10},{15,11},{20,16},{21,... | collective-permute-start | bytes 122888 | tf_op jit(solution)/shard_map/ppermute | solution.py:17
  61.9 3.9 %collective-permute-start.3 = (f32[8,10,1,128]{3,0,2,1:T(8,128)S(1)}, f32[8,10,1,128]{3,0,2,1:T(8,128)S(1)}, u32[]{:S(2)}, u32[]{:S(2)}) collective-permute-start(f32[8,10,1,128]{3,0,2,1:T(8,128)S(1)} %get-tuple-element.80), channel_id=1, source_target_pairs={{0,4},{1,5},{2,6},{3,7},{8,12},{9,13},{10,14},{11,15},{16,20},{17,... | collective-permute-start | bytes 122888 | tf_op jit(solution)/shard_map/ppermute | solution.py:14
  65.8 0.6 copy-start.6
  67.9 8.5 %copy-start.7 = (f32[8,32,128]{2,1,0:T(8,128)S(1)}, f32[8,32,128]{2,1,0:T(8,128)}, u32[]{:S(2)}) copy-start(f32[8,32,128]{2,1,0:T(8,128)} %param.16) | copy-start | bytes 393220
  70.0 7.2 %collective-permute-start.4 = (f32[8,10,34,1]{2,0,3,1:T(8,128)S(1)}, f32[8,10,34,1]{2,0,3,1:T(8,128)S(1)}, u32[]{:S(2)}, u32[]{:S(2)}) collective-permute-start(f32[8,10,34,1]{2,0,3,1:T(8,128)S(1)} %copy.130), channel_id=1, source_target_pairs={{1,0},{2,1},{3,2},{5,4},{6,5},{7,6},{9,8},{10,9},{11,10},{13,12},{... | collective-permute-start | bytes 32648 | tf_op jit(solution)/shard_map/ppermute | solution.py:17
  71.9 6.2 %collective-permute-start.5 = (f32[8,10,34,1]{2,0,3,1:T(8,128)S(1)}, f32[8,10,34,1]{2,0,3,1:T(8,128)S(1)}, u32[]{:S(2)}, u32[]{:S(2)}) collective-permute-start(f32[8,10,34,1]{2,0,3,1:T(8,128)S(1)} %copy.132), channel_id=1, source_target_pairs={{0,1},{1,2},{2,3},{4,5},{5,6},{6,7},{8,9},{9,10},{10,11},{12,13},{... | collective-permute-start | bytes 32648 | tf_op jit(solution)/shard_map/ppermute | solution.py:14
  133.7 7.3 %collective-permute-start.6 = (f32[8,1,32,128]{3,0,2,1:T(8,128)S(1)}, f32[8,1,32,128]{3,0,2,1:T(8,128)S(1)}, u32[]{:S(2)}, u32[]{:S(2)}) collective-permute-start(f32[8,1,32,128]{3,0,2,1:T(8,128)S(1)} %get-tuple-element.83), channel_id=1, source_target_pairs={{8,0},{16,8},{24,16},{9,1},{17,9},{25,17},{10,2},{18,10},{26,18},{... | collective-permute-start | bytes 393224 | tf_op jit(solution)/shard_map/ppermute | solution.py:17
  135.0 7.3 %collective-permute-start.7 = (f32[8,1,32,128]{3,0,2,1:T(8,128)S(1)}, f32[8,1,32,128]{3,0,2,1:T(8,128)S(1)}, u32[]{:S(2)}, u32[]{:S(2)}) collective-permute-start(f32[8,1,32,128]{3,0,2,1:T(8,128)S(1)} %get-tuple-element.82), channel_id=1, source_target_pairs={{0,8},{8,16},{16,24},{1,9},{9,17},{17,25},{2,10},{10,18},{18,26},{... | collective-permute-start | bytes 393224 | tf_op jit(solution)/shard_map/ppermute | solution.py:14
  141.1 6.5 %copy-start.1 = (f32[8,1,32,128]{3,0,2,1:T(8,128)}, f32[8,1,32,128]{3,0,2,1:T(8,128)S(1)}, u32[]{:S(2)}) copy-start(f32[8,1,32,128]{3,0,2,1:T(8,128)S(1)} %collective-permute-done.6) | copy-start | bytes 393220
  142.4 5.2 %copy-start.2 = (f32[8,1,32,128]{3,0,2,1:T(8,128)}, f32[8,1,32,128]{3,0,2,1:T(8,128)S(1)}, u32[]{:S(2)}) copy-start(f32[8,1,32,128]{3,0,2,1:T(8,128)S(1)} %collective-permute-done.7) | copy-start | bytes 393220
  142.4 4.4 %collective-permute-start.8 = (f32[8,10,1,128]{3,0,2,1:T(8,128)S(1)}, f32[8,10,1,128]{3,0,2,1:T(8,128)S(1)}, u32[]{:S(2)}, u32[]{:S(2)}) collective-permute-start(f32[8,10,1,128]{3,0,2,1:T(8,128)S(1)} %get-tuple-element.79), channel_id=1, source_target_pairs={{4,0},{5,1},{6,2},{7,3},{12,8},{13,9},{14,10},{15,11},{20,16},{21,... | collective-permute-start | bytes 122888 | tf_op jit(solution)/shard_map/ppermute | solution.py:17
  143.7 3.9 %collective-permute-start.9 = (f32[8,10,1,128]{3,0,2,1:T(8,128)S(1)}, f32[8,10,1,128]{3,0,2,1:T(8,128)S(1)}, u32[]{:S(2)}, u32[]{:S(2)}) collective-permute-start(f32[8,10,1,128]{3,0,2,1:T(8,128)S(1)} %get-tuple-element.78), channel_id=1, source_target_pairs={{0,4},{1,5},{2,6},{3,7},{8,12},{9,13},{10,14},{11,15},{16,20},{17,... | collective-permute-start | bytes 122888 | tf_op jit(solution)/shard_map/ppermute | solution.py:14
  147.6 0.6 copy-start.5
  152.4 9.4 %collective-permute-start.10 = (f32[8,10,34,1]{2,0,3,1:T(8,128)}, f32[8,10,34,1]{2,0,3,1:T(8,128)}, u32[]{:S(2)}, u32[]{:S(2)}) collective-permute-start(f32[8,10,34,1]{2,0,3,1:T(8,128)} %copy.137), channel_id=1, source_target_pairs={{1,0},{2,1},{3,2},{5,4},{6,5},{7,6},{9,8},{10,9},{11,10},{13,12},{... | collective-permute-start | bytes 32648 | tf_op jit(solution)/shard_map/ppermute | solution.py:17
  155.0 8.3 %collective-permute-start.11 = (f32[8,10,34,1]{2,0,3,1:T(8,128)}, f32[8,10,34,1]{2,0,3,1:T(8,128)}, u32[]{:S(2)}, u32[]{:S(2)}) collective-permute-start(f32[8,10,34,1]{2,0,3,1:T(8,128)} %copy.139), channel_id=1, source_target_pairs={{0,1},{1,2},{2,3},{4,5},{5,6},{6,7},{8,9},{9,10},{10,11},{12,13},{... | collective-permute-start | bytes 32648 | tf_op jit(solution)/shard_map/ppermute | solution.py:14
where the time goes:
time: 229 us; the launch traced here: 228 us
  blocking collectives  127 us (55%)
  starting transfers between devices  33.1 us (14%)
  local copies, waits for them, and re-layouts  22.6 us (10%)
  other arithmetic  21 us (9%)
  matrix products  16.4 us (7%)
  waiting for transfers between devices  6.95 us (3%)
    psum x2, blocking collectives, body(): lax.psum(small_dot(jnp.concatenate([stacked, image], axis=0), image.T), (...  85.1 us
    psum x1, blocking collectives, body(): gram = lax.psum(small_dot(rows, rows.T), ('gx', 'gy', 'gz'))  42 us
    ppermute x6, starting transfers between devices, padded_2(): lax.ppermute(lax.slice_in_dim(block, block.shape[dim] - width, None, axis...  25.4 us
    dot_general x12, matrix products, small_dot(): return jnp.dot(left, right, precision=lax.Precision.HIGHEST)  15.7 us
    ppermute x6, starting transfers between devices, padded_2(): lax.ppermute(lax.slice_in_dim(block, 0, width, axis=dim), axis, backward)  7.73 us
    slice x4, local copies, waits for them, and re-layouts, padded_2(): lax.slice_in_dim(block, 0, width, axis=dim)  7.72 us
    sub x2, other arithmetic, operate(): return (6.0 + shift)[None] * fields - beside  6.01 us
    ppermute x6, waiting for transfers between devices, padded_2(): lax.ppermute(lax.slice_in_dim(block, block.shape[dim] - width, None, axis...  4.75 us
  transfers between devices with their start and end apart: 12, of which 7 were waited for; matrix products, arithmetic and copies ran while one was open for 3% of the time, Pallas kernels for 0%

commit v1 on v0

--- a/solution.py
+++ b/solution.py
@@ -48,9 +48,8 @@
     for step in range(ITERS):
         image = operate(basis[step].reshape(shape), shift).reshape(width, -1)
         stacked = jnp.concatenate(basis, axis=0)
-        products = lax.psum(
-            small_dot(jnp.concatenate([stacked, image], axis=0), image.T), ("gx", "gy", "gz")
-        )
+        load = small_dot(jnp.concatenate([stacked, image], axis=0), image.T)
+        products = jnp.sum(lax.all_gather(load, axis_name=("gx", "gy", "gz")), axis=0)
         coeffs = products[:-width]
         gram = products[-width:] - small_dot(coeffs.T, coeffs)
         projected = image - small_dot(coeffs.T, stacked)

time: 229 us -> 279 us (1.22)
  blocking collectives: 127 us -> 177 us
    all_gather x0 -> x2, blocking collectives: none -> 135 us  [body(): lax.all_gather(load, axis_name=('gx', 'gy', 'gz'))]
    psum x2 -> x0, blocking collectives: 85.1 us -> none  [body(): lax.psum(small_dot(jnp.concatenate([stacked, image], axis=0), image.T), (...]
  transfers between devices with their start and end apart: 12 -> 12, of which waited for: 7 -> 7; matrix products, arithmetic and copies ran while one was open for 3% -> 2% of each run, Pallas kernels for 0% -> 0%
where the time goes in v1:
time: 279 us; the launch traced here: 278 us
  blocking collectives  177 us (63%)
  starting transfers between devices  32.9 us (12%)
  local copies, waits for them, and re-layouts  22.6 us (8%)
  other arithmetic  21.1 us (8%)
  matrix products  16.1 us (6%)
  waiting for transfers between devices  6.95 us (2%)
    all_gather x2, blocking collectives, body(): lax.all_gather(load, axis_name=('gx', 'gy', 'gz'))  135 us
    psum x1, blocking collectives, body(): gram = lax.psum(small_dot(rows, rows.T), ('gx', 'gy', 'gz'))  42 us
    ppermute x6, starting transfers between devices, padded_2(): lax.ppermute(lax.slice_in_dim(block, block.shape[dim] - width, None, axis...  25.1 us
    dot_general x12, matrix products, small_dot(): return jnp.dot(left, right, precision=lax.Precision.HIGHEST)  15.5 us
    ppermute x6, starting transfers between devices, padded_2(): lax.ppermute(lax.slice_in_dim(block, 0, width, axis=dim), axis, backward)  7.73 us
    slice x4, local copies, waits for them, and re-layouts, padded_2(): lax.slice_in_dim(block, 0, width, axis=dim)  7.72 us
    sub x2, other arithmetic, operate(): return (6.0 + shift)[None] * fields - beside  6.01 us
  transfers between devices with their start and end apart: 12, of which 7 were waited for; matrix products, arithmetic and copies ran while one was open for 2% of the time, Pallas kernels for 0%

profile of v1, /device:TPU:0, one launch (start us, length us, event | category | flops | bytes accessed | tf_op | source)
XLA Modules:
  0.0 278.0 jit_solution(10991202681598207511)
XLA Ops:
  0.6 4.6 %convolution_bitcast_fusion = f32[8,8]{0,1:T(8,128)S(1)} fusion(f32[8,8,32,128]{3,2,1,0:T(8,128)} %param.15), kind=kOutput, calls=%fused_computation.21 | convolution fusion | flops 25165824 | bytes 1048832 | tf_op jit(solution)/shard_map/dot_general | solution.py:36
  5.2 42.0 %psum.7 = f32[8,8]{0,1:T(8,128)S(1)} all-reduce(f32[8,8]{0,1:T(8,128)S(1)} %convolution_bitcast_fusion), channel_id=1, replica_groups=mesh['gx'=4,'gy'=2,'gz'=4] {'gx','gy','gz'}, use_global_device_ids=true, to_apply=%region_0.0 | all-reduce | flops 64 | bytes 512 | tf_op jit(solution)/shard_map/psum | solution.py:43
  50.2 1.5 fusion.16
  51.7 1.3 collective-permute-start
  53.0 4.8 %collective-permute-start.1 = (f32[8,1,32,128]{3,0,2,1:T(8,128)S(1)}, f32[8,1,32,128]{3,0,2,1:T(8,128)S(1)}, u32[]{:S(2)}, u32[]{:S(2)}) collective-permute-start(f32[8,1,32,128]{3,0,2,1:T(8,128)S(1)} %get-tuple-element.84), channel_id=1, source_target_pairs={{0,8},{8,16},{16,24},{1,9},{9,17},{17,25},{2,10},{10,18},{18,26},{... | collective-permute-start | bytes 393224 | tf_op jit(solution)/shard_map/ppermute | solution.py:14
  58.8 1.5 collective-permute-done.1
  60.3 1.3 collective-permute-start.2
  61.6 3.0 %collective-permute-start.3 = (f32[8,10,1,128]{3,0,2,1:T(8,128)S(1)}, f32[8,10,1,128]{3,0,2,1:T(8,128)S(1)}, u32[]{:S(2)}, u32[]{:S(2)}) collective-permute-start(f32[8,10,1,128]{3,0,2,1:T(8,128)S(1)} %get-tuple-element.80), channel_id=1, source_target_pairs={{0,4},{1,5},{2,6},{3,7},{8,12},{9,13},{10,14},{11,15},{16,20},{17,... | collective-permute-start | bytes 122888 | tf_op jit(solution)/shard_map/ppermute | solution.py:14
  66.1 1.5 fusion.60
  67.7 2.0 copy.130
  69.7 1.3 collective-permute-start.4
  71.7 4.5 %collective-permute-start.5 = (f32[8,10,34,1]{2,0,3,1:T(8,128)S(1)}, f32[8,10,34,1]{2,0,3,1:T(8,128)S(1)}, u32[]{:S(2)}, u32[]{:S(2)}) collective-permute-start(f32[8,10,34,1]{2,0,3,1:T(8,128)S(1)} %copy.132), channel_id=1, source_target_pairs={{0,1},{1,2},{2,3},{4,5},{5,6},{6,7},{8,9},{9,10},{10,11},{12,13},{... | collective-permute-start | bytes 32648 | tf_op jit(solution)/shard_map/ppermute | solution.py:14
  77.9 1.8 copy.133
  79.6 3.0 %fusion.26 = f32[8,8,32,128]{3,0,2,1:T(8,128)S(1)} fusion(f32[8,10,34,1]{3,0,2,1:T(8,128)} %copy.133, f32[8,10,1,128]{3,0,2,1:T(8,128)S(1)} %collective-permute-done.2, f32[8,10,1,128]{3,0,2,1:T(8,128)} %copy-done.6, f32[8,1,32,128]{3,0,2,1:T(8,128)} %copy-done.3, f32[8,8,32,128]{3,0,2,1:T(8,128)S(1)} %bitcast.77, f32[8,1,32,128]{3,0,2,1:T(8,128)} %copy-done.4, ...), kind=kLoop, calls=%fused_computation.52 | loop fusion | flops 6553600 | bytes 2594048 | tf_op jit(solution)/shard_map/sub | solution.py:27
  82.7 2.6 fusion.10
  85.2 70.5 %all-gather.2 = f32[32,16,8]{1,2,0:T(8,128)S(1)} all-gather(f32[1,16,8]{1,2,0:T(8,128)S(1)} %fusion.10), channel_id=2, replica_groups=mesh['gx'=4,'gy'=2,'gz'=4] {'gx','gy','gz'}, dimensions={0}, use_global_device_ids=true | all-gather | bytes 16896 | tf_op jit(solution)/shard_map/all_gather | solution.py:52
  160.8 1.3 collective-permute-start.6
  162.1 4.6 %collective-permute-start.7 = (f32[8,1,32,128]{3,0,2,1:T(8,128)S(1)}, f32[8,1,32,128]{3,0,2,1:T(8,128)S(1)}, u32[]{:S(2)}, u32[]{:S(2)}) collective-permute-start(f32[8,1,32,128]{3,0,2,1:T(8,128)S(1)} %get-tuple-element.82), channel_id=1, source_target_pairs={{0,8},{8,16},{16,24},{1,9},{9,17},{17,25},{2,10},{10,18},{18,26},{... | collective-permute-start | bytes 393224 | tf_op jit(solution)/shard_map/ppermute | solution.py:14
  167.7 1.5 collective-permute-done.7
  169.2 1.3 collective-permute-start.8
  170.5 3.0 %collective-permute-start.9 = (f32[8,10,1,128]{3,0,2,1:T(8,128)S(1)}, f32[8,10,1,128]{3,0,2,1:T(8,128)S(1)}, u32[]{:S(2)}, u32[]{:S(2)}) collective-permute-start(f32[8,10,1,128]{3,0,2,1:T(8,128)S(1)} %get-tuple-element.78), channel_id=1, source_target_pairs={{0,4},{1,5},{2,6},{3,7},{8,12},{9,13},{10,14},{11,15},{16,20},{17,... | collective-permute-start | bytes 122888 | tf_op jit(solution)/shard_map/ppermute | solution.py:14
  175.1 1.5 fusion.59
  176.6 2.6 copy.137
  181.8 5.2 %collective-permute-start.11 = (f32[8,10,34,1]{2,0,3,1:T(8,128)}, f32[8,10,34,1]{2,0,3,1:T(8,128)}, u32[]{:S(2)}, u32[]{:S(2)}) collective-permute-start(f32[8,10,34,1]{2,0,3,1:T(8,128)} %copy.139), channel_id=1, source_target_pairs={{0,1},{1,2},{2,3},{4,5},{5,6},{6,7},{8,9},{9,10},{10,11},{12,13},{... | collective-permute-start | bytes 32648 | tf_op jit(solution)/shard_map/ppermute | solution.py:14
  188.7 1.5 copy.138
  190.1 2.6 copy.140
  192.7 3.0 %fusion.20 = f32[8,8,32,128]{3,0,2,1:T(8,128)S(1)} fusion(f32[8,10,34,1]{3,0,2,1:T(8,128)} %copy.140, f32[8,10,1,128]{3,0,2,1:T(8,128)S(1)} %collective-permute-done.8, f32[8,10,1,128]{3,0,2,1:T(8,128)} %copy-done.5, f32[8,1,32,128]{3,0,2,1:T(8,128)} %copy-done.1, f32[8,8,32,128]{3,0,2,1:T(8,128)S(1)} %bitcast.81, f32[8,1,32,128]{3,0,2,1:T(8,128)} %copy-done.2, ...), kind=kLoop, calls=%fused_computation.28 | loop fusion | flops 6553600 | bytes 2594048 | tf_op jit(solution)/shard_map/sub | solution.py:27
  195.7 3.0 %fusion.11 = f32[1,24,8]{1,2,0:T(8,128)S(1)} fusion(f32[8,32768]{1,0:T(8,128)S(1)} %bitcast.86, f32[8,32768]{1,0:T(8,128)S(1)} %fusion.64, f32[8,32768]{1,0:T(8,128)S(1)} %fusion.16), kind=kOutput, calls=%fused_computation.16 | convolution fusion | flops 77070336 | bytes 3146496 | tf_op jit(solution)/shard_map/dot_general | solution.py:36
  198.7 65.0 %all-gather.3 = f32[32,24,8]{1,2,0:T(8,128)S(1)} all-gather(f32[1,24,8]{1,2,0:T(8,128)S(1)} %fusion.11), channel_id=3, replica_groups=mesh['gx'=4,'gy'=2,'gz'=4] {'gx','gy','gz'}, dimensions={0}, use_global_device_ids=true | all-gather | bytes 25344 | tf_op jit(solution)/shard_map/all_gather | solution.py:52
  266.0 2.0 dynamic-slice_select_fusion
  268.0 1.7 scatter.20
  270.5 1.5 cholesky.41
  (85 shorter events, 28.7 us)
Async XLA Ops:
  0.6 49.5 %copy-start = (f32[8,8,32,128]{3,2,1,0:T(8,128)S(1)}, f32[8,8,32,128]{3,2,1,0:T(8,128)}, u32[]{:S(2)}) copy-start(f32[8,8,32,128]{3,2,1,0:T(8,128)} %param.15) | copy-start | bytes 3145732
  51.7 7.1 %collective-permute-start = (f32[8,1,32,128]{3,0,2,1:T(8,128)S(1)}, f32[8,1,32,128]{3,0,2,1:T(8,128)S(1)}, u32[]{:S(2)}, u32[]{:S(2)}) collective-permute-start(f32[8,1,32,128]{3,0,2,1:T(8,128)S(1)} %get-tuple-element.85), channel_id=1, source_target_pairs={{8,0},{16,8},{24,16},{9,1},{17,9},{25,17},{10,2},{18,10},{26,18},{... | collective-permute-start | bytes 393224 | tf_op jit(solution)/shard_map/ppermute | solution.py:17
  53.0 7.3 %collective-permute-start.1 = (f32[8,1,32,128]{3,0,2,1:T(8,128)S(1)}, f32[8,1,32,128]{3,0,2,1:T(8,128)S(1)}, u32[]{:S(2)}, u32[]{:S(2)}) collective-permute-start(f32[8,1,32,128]{3,0,2,1:T(8,128)S(1)} %get-tuple-element.84), channel_id=1, source_target_pairs={{0,8},{8,16},{16,24},{1,9},{9,17},{17,25},{2,10},{10,18},{18,26},{... | collective-permute-start | bytes 393224 | tf_op jit(solution)/shard_map/ppermute | solution.py:14
  58.8 6.8 %copy-start.3 = (f32[8,1,32,128]{3,0,2,1:T(8,128)}, f32[8,1,32,128]{3,0,2,1:T(8,128)S(1)}, u32[]{:S(2)}) copy-start(f32[8,1,32,128]{3,0,2,1:T(8,128)S(1)} %collective-permute-done) | copy-start | bytes 393220
  60.3 5.3 %copy-start.4 = (f32[8,1,32,128]{3,0,2,1:T(8,128)}, f32[8,1,32,128]{3,0,2,1:T(8,128)S(1)}, u32[]{:S(2)}) copy-start(f32[8,1,32,128]{3,0,2,1:T(8,128)S(1)} %collective-permute-done.1) | copy-start | bytes 393220
  60.3 4.3 %collective-permute-start.2 = (f32[8,10,1,128]{3,0,2,1:T(8,128)S(1)}, f32[8,10,1,128]{3,0,2,1:T(8,128)S(1)}, u32[]{:S(2)}, u32[]{:S(2)}) collective-permute-start(f32[8,10,1,128]{3,0,2,1:T(8,128)S(1)} %get-tuple-element.81), channel_id=1, source_target_pairs={{4,0},{5,1},{6,2},{7,3},{12,8},{13,9},{14,10},{15,11},{20,16},{21,... | collective-permute-start | bytes 122888 | tf_op jit(solution)/shard_map/ppermute | solution.py:17
  61.6 3.9 %collective-permute-start.3 = (f32[8,10,1,128]{3,0,2,1:T(8,128)S(1)}, f32[8,10,1,128]{3,0,2,1:T(8,128)S(1)}, u32[]{:S(2)}, u32[]{:S(2)}) collective-permute-start(f32[8,10,1,128]{3,0,2,1:T(8,128)S(1)} %get-tuple-element.80), channel_id=1, source_target_pairs={{0,4},{1,5},{2,6},{3,7},{8,12},{9,13},{10,14},{11,15},{16,20},{17,... | collective-permute-start | bytes 122888 | tf_op jit(solution)/shard_map/ppermute | solution.py:14
  65.5 0.6 copy-start.6
  67.7 8.5 %copy-start.7 = (f32[8,32,128]{2,1,0:T(8,128)S(1)}, f32[8,32,128]{2,1,0:T(8,128)}, u32[]{:S(2)}) copy-start(f32[8,32,128]{2,1,0:T(8,128)} %param.16) | copy-start | bytes 393220
  69.7 7.2 %collective-permute-start.4 = (f32[8,10,34,1]{2,0,3,1:T(8,128)S(1)}, f32[8,10,34,1]{2,0,3,1:T(8,128)S(1)}, u32[]{:S(2)}, u32[]{:S(2)}) collective-permute-start(f32[8,10,34,1]{2,0,3,1:T(8,128)S(1)} %copy.130), channel_id=1, source_target_pairs={{1,0},{2,1},{3,2},{5,4},{6,5},{7,6},{9,8},{10,9},{11,10},{13,12},{... | collective-permute-start | bytes 32648 | tf_op jit(solution)/shard_map/ppermute | solution.py:17
  71.7 6.2 %collective-permute-start.5 = (f32[8,10,34,1]{2,0,3,1:T(8,128)S(1)}, f32[8,10,34,1]{2,0,3,1:T(8,128)S(1)}, u32[]{:S(2)}, u32[]{:S(2)}) collective-permute-start(f32[8,10,34,1]{2,0,3,1:T(8,128)S(1)} %copy.132), channel_id=1, source_target_pairs={{0,1},{1,2},{2,3},{4,5},{5,6},{6,7},{8,9},{9,10},{10,11},{12,13},{... | collective-permute-start | bytes 32648 | tf_op jit(solution)/shard_map/ppermute | solution.py:14
  160.8 6.9 %collective-permute-start.6 = (f32[8,1,32,128]{3,0,2,1:T(8,128)S(1)}, f32[8,1,32,128]{3,0,2,1:T(8,128)S(1)}, u32[]{:S(2)}, u32[]{:S(2)}) collective-permute-start(f32[8,1,32,128]{3,0,2,1:T(8,128)S(1)} %get-tuple-element.83), channel_id=1, source_target_pairs={{8,0},{16,8},{24,16},{9,1},{17,9},{25,17},{10,2},{18,10},{26,18},{... | collective-permute-start | bytes 393224 | tf_op jit(solution)/shard_map/ppermute | solution.py:17
  162.1 7.1 %collective-permute-start.7 = (f32[8,1,32,128]{3,0,2,1:T(8,128)S(1)}, f32[8,1,32,128]{3,0,2,1:T(8,128)S(1)}, u32[]{:S(2)}, u32[]{:S(2)}) collective-permute-start(f32[8,1,32,128]{3,0,2,1:T(8,128)S(1)} %get-tuple-element.82), channel_id=1, source_target_pairs={{0,8},{8,16},{16,24},{1,9},{9,17},{17,25},{2,10},{10,18},{18,26},{... | collective-permute-start | bytes 393224 | tf_op jit(solution)/shard_map/ppermute | solution.py:14
  167.7 6.7 %copy-start.1 = (f32[8,1,32,128]{3,0,2,1:T(8,128)}, f32[8,1,32,128]{3,0,2,1:T(8,128)S(1)}, u32[]{:S(2)}) copy-start(f32[8,1,32,128]{3,0,2,1:T(8,128)S(1)} %collective-permute-done.6) | copy-start | bytes 393220
  169.2 5.2 %copy-start.2 = (f32[8,1,32,128]{3,0,2,1:T(8,128)}, f32[8,1,32,128]{3,0,2,1:T(8,128)S(1)}, u32[]{:S(2)}) copy-start(f32[8,1,32,128]{3,0,2,1:T(8,128)S(1)} %collective-permute-done.7) | copy-start | bytes 393220
  169.2 4.4 %collective-permute-start.8 = (f32[8,10,1,128]{3,0,2,1:T(8,128)S(1)}, f32[8,10,1,128]{3,0,2,1:T(8,128)S(1)}, u32[]{:S(2)}, u32[]{:S(2)}) collective-permute-start(f32[8,10,1,128]{3,0,2,1:T(8,128)S(1)} %get-tuple-element.79), channel_id=1, source_target_pairs={{4,0},{5,1},{6,2},{7,3},{12,8},{13,9},{14,10},{15,11},{20,16},{21,... | collective-permute-start | bytes 122888 | tf_op jit(solution)/shard_map/ppermute | solution.py:17
  170.5 3.9 %collective-permute-start.9 = (f32[8,10,1,128]{3,0,2,1:T(8,128)S(1)}, f32[8,10,1,128]{3,0,2,1:T(8,128)S(1)}, u32[]{:S(2)}, u32[]{:S(2)}) collective-permute-start(f32[8,10,1,128]{3,0,2,1:T(8,128)S(1)} %get-tuple-element.78), channel_id=1, source_target_pairs={{0,4},{1,5},{2,6},{3,7},{8,12},{9,13},{10,14},{11,15},{16,20},{17,... | collective-permute-start | bytes 122888 | tf_op jit(solution)/shard_map/ppermute | solution.py:14
  174.4 0.6 copy-start.5
  179.3 9.4 %collective-permute-start.10 = (f32[8,10,34,1]{2,0,3,1:T(8,128)}, f32[8,10,34,1]{2,0,3,1:T(8,128)}, u32[]{:S(2)}, u32[]{:S(2)}) collective-permute-start(f32[8,10,34,1]{2,0,3,1:T(8,128)} %copy.137), channel_id=1, source_target_pairs={{1,0},{2,1},{3,2},{5,4},{6,5},{7,6},{9,8},{10,9},{11,10},{13,12},{... | collective-permute-start | bytes 32648 | tf_op jit(solution)/shard_map/ppermute | solution.py:17
  181.8 8.3 %collective-permute-start.11 = (f32[8,10,34,1]{2,0,3,1:T(8,128)}, f32[8,10,34,1]{2,0,3,1:T(8,128)}, u32[]{:S(2)}, u32[]{:S(2)}) collective-permute-start(f32[8,10,34,1]{2,0,3,1:T(8,128)} %copy.139), channel_id=1, source_target_pairs={{0,1},{1,2},{2,3},{4,5},{5,6},{6,7},{8,9},{9,10},{10,11},{12,13},{... | collective-permute-start | bytes 32648 | tf_op jit(solution)/shard_map/ppermute | solution.py:14
